TPU v7x, 32 devices: a whole 2x2x4 slice. The times are simulated.
32 devices in a mesh: seq: 8 (over z, y), batch: 4 (over x, core).
Axes of the slice: x: 2, y: 2, z: 4, core: 2. Of those that a mesh axis runs over, the one named last changes fastest.
Arguments:
- tokens: bfloat16 [4, 8192, 1024], P('batch', 'seq'), may hold values from -6 to 6
- logits: bfloat16 [4, 8192, 256], P('batch', 'seq'), may hold values from -160 to 160
- slot_grad: bfloat16 [4, 256, 1024], P('batch', 'seq'), may hold values from -6 to 6
- phi_param: bfloat16 [1024, 256], P('seq'), may hold values from -0.1875 to 0.1875
Outputs:
- token_grad: bfloat16 [4, 8192, 1024], P('batch', 'seq')
- phi_grad: float32 [1024, 256], P('seq')
All inputs are finite; a program needn't handle non-finite values.
Results may differ from a plain program's by a relative error of at most 0.0049.
Values may be sent and summed in bfloat16 or wider, within the bound.
A program may use at most 64 MiB of HBM per device.

v0:
```python
import functools

import jax
import jax.numpy as jnp
from jax import lax
from jax.experimental import pallas as pl
from jax.experimental.pallas import tpu as pltpu
from jax.sharding import PartitionSpec as P

MESH = pl.DeviceIdType.MESH
F32 = jnp.float32
BF16 = jnp.bfloat16


def fused_kernel(
    n, scale, tok_hbm, log_hbm, slot_hbm, phi_hbm, tok_out, phi_out,
    tok, log, raw, wg, gath, phig, stat, disp, lg, tokt, part, part_low, recv_a, sum_a, low_a,
    recv_b, sum_b, low_b, recv_c, fin,
    load_sem, ag_send, ag_recv, fw_send, fw_recv, st_send, st_recv, ph_send, ph_recv,
    pb_send, pb_recv, a_send, a_recv, b_send, b_recv, c_send, c_recv, d_send, d_recv,
):
    me = lax.axis_index("seq")
    bat = lax.axis_index("batch")
    half = n // 2
    twin = me + 1 - 2 * (me % 2)
    bat_a = bat + 1 - 2 * (bat % 2)
    bat_b = (bat + 2) % 4
    bat_c = (bat_a + 2) % 4
    keep_a = bat % 2
    keep_b = bat // 2
    rows = tok.shape[0]
    step = min(256, rows)
    steps = rows // step

    def remote(src, dst, send, recv, seq_at, bat_at):
        return pltpu.make_async_remote_copy(
            src_ref=src, dst_ref=dst, send_sem=send, recv_sem=recv,
            device_id=(seq_at, bat_at), device_id_type=MESH,
        )

    load_slot = pltpu.make_async_copy(slot_hbm, gath.at[me], load_sem.at[0])
    load_log = pltpu.make_async_copy(log_hbm, log, load_sem.at[1])
    load_phi = pltpu.make_async_copy(phi_hbm.at[bat], phig.at[me, bat], load_sem.at[2])
    load_tok = pltpu.make_async_copy(tok_hbm, tok, load_sem.at[3])
    load_slot.start()
    load_log.start()
    load_tok.start()
    load_phi.start()

    barrier = pltpu.get_barrier_semaphore()
    for k in range(1, n):
        pl.semaphore_signal(barrier, inc=1, device_id=((me + k) % n, bat), device_id_type=MESH)
    for other in (bat_a, bat_b, bat_c):
        pl.semaphore_signal(barrier, inc=1, device_id=(me, other), device_id_type=MESH)
    pl.semaphore_wait(barrier, n - 1 + 3)

    load_slot.wait()
    pieces = 2 if gath.shape[1] % 32 == 0 else 1
    piece = gath.shape[1] // pieces

    def shard(j, h):
        return gath.at[j, pl.ds(h * piece, piece)]

    place = me // 2
    low = 1 - place // (half // 2)

    def column_peer(i):
        at = low * (half - 1 - i) + (1 - low) * i
        return at - low * ((place - at + half) // half) + (1 - low) * ((at - place + half) // half)

    to_twin = []
    direct = []
    for h in range(pieces):
        to_twin.append(remote(shard(me, h), shard(me, h), fw_send.at[0, h], fw_recv.at[me // 2, h], twin, bat))
        to_twin[-1].start()
        for k in range(1, half):
            target = column_peer(k - 1)
            direct.append(remote(
                shard(me, h), shard(me, h), ag_send.at[k, h], ag_recv.at[me // 2, h], 2 * target + me % 2, bat))
            direct[-1].start()

    load_log.wait()

    def chunk(i):
        return pl.ds(pl.multiple_of(i * step, step), step)

    def peak_step(i, top):
        return jnp.maximum(top, jnp.max(log[chunk(i), :].astype(F32), axis=0, keepdims=True))

    slots = log.shape[1]
    peak = lax.fori_loop(0, steps, peak_step, jnp.full((1, slots), -jnp.inf, F32))

    def exp_step(i, acc):
        values = jnp.exp(log[chunk(i), :].astype(F32) - peak)
        raw[chunk(i), :] = values
        return acc + jnp.sum(values, axis=0, keepdims=True)

    total = lax.fori_loop(0, steps, exp_step, jnp.zeros((1, slots), F32))

    load_tok.wait()

    def turn_step(i, carry):
        tokt[:, chunk(i)] = tok[chunk(i), :].T
        return carry

    lax.fori_loop(0, steps, turn_step, 0)
    relayed = []
    for h in range(pieces):
        for k in range(1, half):
            origin = column_peer(k - 1)
            source = 2 * origin + me % 2
            remote(shard(source, h), shard(source, h), ag_send.at[k, h], ag_recv.at[origin, h], source, bat).wait_recv()
            relayed.append(
                remote(shard(source, h), shard(source, h), fw_send.at[k, h], fw_recv.at[origin, h], twin, bat))
            relayed[-1].start()
    for h in range(pieces):
        for j in range(half):
            source = 2 * j + twin % 2
            remote(shard(source, h), shard(source, h), fw_send.at[0, h], fw_recv.at[j, h], twin, bat).wait_recv()

    upstream = gath.reshape(slots, gath.shape[2])

    large = 2 * step if rows % (2 * step) == 0 else step

    def wide(i):
        return pl.ds(pl.multiple_of(i * large, large), large)

    def wg_step(i, acc):
        values = lax.dot_general(
            tok[wide(i), :], upstream[...], (((1,), (1,)), ((), ())), preferred_element_type=F32
        )
        wg[wide(i), :] = values
        return acc + jnp.sum(values * raw[wide(i), :], axis=0, keepdims=True)

    dot = lax.fori_loop(0, rows // large, wg_step, jnp.zeros((1, slots), F32))

    stat[me, 0:1, :] = peak
    stat[me, 1:2, :] = total
    stat[me, 2:3, :] = dot
    stat_moves = []
    for k in range(1, n):
        stat_moves.append(remote(stat.at[me], stat.at[me], st_send.at[k], st_recv.at[k], (me + k) % n, bat))
        stat_moves[-1].start()

    load_phi.wait()
    phi_moves = []
    for k in range(1, n):
        phi_moves.append(remote(phig.at[me, bat], phig.at[me, bat], ph_send.at[k], ph_recv.at[k], (me + k) % n, bat))
        phi_moves[-1].start()

    for move in stat_moves:
        move.wait_recv()
    peaks = stat[:, 0, :]
    col_peak = jnp.max(peaks, axis=0, keepdims=True)
    shifts = jnp.exp(peaks - col_peak)
    col_total = jnp.sum(stat[:, 1, :] * shifts, axis=0, keepdims=True)
    col_dot = jnp.sum(stat[:, 2, :] * shifts, axis=0, keepdims=True) / col_total
    factor = jnp.exp(peak - col_peak) / col_total

    def grad_step(i, carry):
        weights = raw[chunk(i), :] * factor
        grads = weights * (wg[chunk(i), :] - col_dot)
        disp[chunk(i), :] = weights.astype(BF16)
        lg[chunk(i), :] = grads.astype(BF16)
        return carry

    lax.fori_loop(0, steps, grad_step, 0)

    own = tok.shape[1] // n
    quarter = own // 4

    group = n // 2
    owners = [[j for j in range(n) if (n // 4 <= j < n - n // 4) == bool(g)] for g in range(2)]
    moves_a = []
    for g in range(2):
        for at in range(0, group, 2):
            j = owners[g][at]
            terms = jnp.dot(tokt[own * j : own * (j + 2), :], lg[...], preferred_element_type=F32)
            for side in range(2):
                for qa in range(2):
                    for qb in range(2):
                        first = own * side + (2 * qa + qb) * quarter
                        block = terms[first : first + quarter, :]
                        part[g, qa, qb, at + side] = block
                        part_low[g, qa, qb, at + side] = block.astype(BF16)
        moves_a.append(remote(part_low.at[g, 1 - keep_a], recv_a.at[g], a_send.at[g], a_recv.at[g], me, bat_a))
        moves_a[-1].start()
    moves_b = []
    for g in range(2):
        moves_a[g].wait_recv()
        for qb in range(2):
            for at in range(group):
                block = part[g, keep_a, qb, at] + recv_a[g, qb, at].astype(F32)
                sum_a[g, qb, at] = block
                low_a[g, qb, at] = block.astype(BF16)
        moves_b.append(remote(low_a.at[g, 1 - keep_b], recv_b.at[g], b_send.at[g], b_recv.at[g], me, bat_b))
        moves_b[-1].start()
    for move in phi_moves:
        move.wait_recv()
    phi_b = remote(phig.at[:, bat], phig.at[:, bat], pb_send.at[0], pb_recv.at[0], me, bat_b)
    phi_b.start()

    def share_move(g, at):
        j = owners[g][at]
        return remote(low_b.at[g, at], recv_c.at[me], c_send.at[j], c_recv.at[me], j, bat)

    for g in range(2):
        moves_b[g].wait_recv()
        for at in range(group):
            block = sum_a[g, keep_b, at] + recv_b[g, at].astype(F32)
            sum_b[owners[g][at]] = block
            low_b[g, at] = block.astype(BF16)
        for at in range(group):
            @pl.when(me != owners[g][at])
            def _(g=g, at=at):
                share_move(g, at).start()

    phi_b.wait_recv()
    phi_a = [
        remote(phig.at[:, bat], phig.at[:, bat], pb_send.at[1], pb_recv.at[1], me, bat_a),
        remote(phig.at[:, bat_b], phig.at[:, bat_b], pb_send.at[2], pb_recv.at[2], me, bat_a),
    ]
    for move in phi_a:
        move.start()
    share = sum_b[me]
    for k in range(1, n):
        source = (me - k + n) % n
        remote(low_b.at[0, 0], recv_c.at[source], c_send.at[0], c_recv.at[source], source, bat).wait_recv()
        share = share + recv_c[source].astype(F32)
    mine = 2 * keep_a + keep_b
    fin[mine] = share
    last = []
    for k, other in enumerate((bat_c, bat_b, bat_a)):
        last.append(remote(fin.at[mine], fin.at[mine], d_send.at[k], d_recv.at[k], me, other))
        last[-1].start()
    for move in phi_a:
        move.wait_recv()

    phi_full = phig.reshape(phig.shape[0] * phig.shape[1] * phig.shape[2], phig.shape[3])

    def out_step(i, carry):
        values = jnp.dot(disp[wide(i), :], upstream[...], preferred_element_type=F32)
        values = values + lax.dot_general(
            lg[wide(i), :], phi_full[...], (((1,), (1,)), ((), ())), preferred_element_type=F32
        )
        tok_out[wide(i), :] = (scale * values).astype(BF16)
        return carry

    lax.fori_loop(0, rows // large, out_step, 0)

    for move in last:
        move.wait_recv()
    phi_out[...] = fin[...].reshape(own, slots)

    for g in range(2):
        for at in range(group):
            @pl.when(me != owners[g][at])
            def _(g=g, at=at):
                share_move(g, at).wait_send()
    for move in to_twin + direct + relayed + stat_moves + phi_moves + moves_a + moves_b + [phi_b] + phi_a + last:
        move.wait_send()


def fused(n, tokens, logits, slot_grad, phi_param):
    rows, width = tokens.shape
    slots = logits.shape[1]
    own = width // n
    scale = float(n * rows // 16)
    dma = pltpu.SemaphoreType.DMA
    hbm = pl.BlockSpec(memory_space=pltpu.HBM)
    return pl.pallas_call(
        functools.partial(fused_kernel, n, scale),
        out_shape=(
            jax.ShapeDtypeStruct((rows, width), BF16),
            jax.ShapeDtypeStruct((own, slots), F32),
        ),
        in_specs=[hbm] * 4,
        out_specs=(pl.BlockSpec(memory_space=pltpu.VMEM), pl.BlockSpec(memory_space=pltpu.VMEM)),
        scratch_shapes=[
            pltpu.VMEM((rows, width), BF16),
            pltpu.VMEM((rows, slots), BF16),
            pltpu.VMEM((rows, slots), F32),
            pltpu.VMEM((rows, slots), F32),
            pltpu.VMEM((n, slots // n, width), BF16),
            pltpu.VMEM((n, 4, own // 4, slots), BF16),
            pltpu.VMEM((n, 8, slots), F32),
            pltpu.VMEM((rows, slots), BF16),
            pltpu.VMEM((rows, slots), BF16),
            pltpu.VMEM((width, rows), BF16),
            pltpu.VMEM((2, 2, 2, n // 2, own // 4, slots), F32),
            pltpu.VMEM((2, 2, 2, n // 2, own // 4, slots), BF16),
            pltpu.VMEM((2, 2, n // 2, own // 4, slots), BF16),
            pltpu.VMEM((2, 2, n // 2, own // 4, slots), F32),
            pltpu.VMEM((2, 2, n // 2, own // 4, slots), BF16),
            pltpu.VMEM((2, n // 2, own // 4, slots), BF16),
            pltpu.VMEM((n, own // 4, slots), F32),
            pltpu.VMEM((2, n // 2, own // 4, slots), BF16),
            pltpu.VMEM((n, own // 4, slots), BF16),
            pltpu.VMEM((4, own // 4, slots), F32),
            dma((4,)),
            dma((n // 2, 2)), dma((n // 2, 2)),
            dma((n // 2, 2)), dma((n // 2, 2)),
            dma((n,)), dma((n,)),
            dma((n,)), dma((n,)),
            dma((3,)), dma((3,)),
            dma((2,)), dma((2,)),
            dma((2,)), dma((2,)),
            dma((n,)), dma((n,)),
            dma((3,)), dma((3,)),
        ],
        compiler_params=pltpu.CompilerParams(
            collective_id=0, has_side_effects=True, vmem_limit_bytes=52_000_000
        ),
    )(*[
        pltpu.with_memory_space_constraint(x, pltpu.HBM)
        for x in (tokens, logits, slot_grad, phi_param.reshape(4, own // 4, slots))
    ])


def plain(tokens, logits, slot_grad, phi_param):
    inputs = tokens[0]
    scores = logits[0].astype(jnp.float32)
    upstream, phi_full = (
        lax.all_gather(slot_grad[0], "seq", axis=0, tiled=True),
        lax.all_gather(phi_param, "seq", axis=0, tiled=True),
    )
    weight_grad = lax.dot_general(
        inputs, upstream, (((1,), (1,)), ((), ())), preferred_element_type=jnp.float32
    )
    col_peak = lax.pmax(jnp.max(scores, axis=0, keepdims=True), "seq")
    raw_weights = jnp.exp(scores - col_peak)
    col_total = lax.psum(jnp.sum(raw_weights, axis=0, keepdims=True), "seq")
    dispatch = raw_weights / col_total
    col_dot = lax.psum(jnp.sum(dispatch * weight_grad, axis=0, keepdims=True), "seq")
    logit_grad = (dispatch * (weight_grad - col_dot)).astype(jnp.bfloat16)
    dispatch_low = dispatch.astype(jnp.bfloat16)
    grad_scale = float(lax.axis_size("seq") * inputs.shape[0] // 16)
    token_sum = jnp.dot(dispatch_low, upstream, preferred_element_type=jnp.float32)
    token_sum = token_sum + lax.dot_general(
        logit_grad, phi_full, (((1,), (1,)), ((), ())), preferred_element_type=jnp.float32
    )
    token_grad = (grad_scale * token_sum).astype(jnp.bfloat16)[None]
    phi_terms = lax.dot_general(
        inputs, logit_grad, (((0,), (0,)), ((), ())), preferred_element_type=jnp.float32
    )
    phi_share = lax.psum_scatter(phi_terms, "seq", scatter_dimension=0, tiled=True)
    phi_grad = lax.psum(phi_share, "batch")
    return (token_grad, phi_grad)


def per_device(n, batches, tokens, logits, slot_grad, phi_param):
    own, slots = phi_param.shape
    if batches == 4 and n % 8 == 0 and slot_grad.shape[1] % 16 == 0 and own % 128 == 0 and slots % 128 == 0 and tokens.shape[1] % 256 == 0:
        token_grad, phi_grad = fused(n, tokens[0], logits[0], slot_grad[0], phi_param)
        return token_grad[None], phi_grad
    return plain(tokens, logits, slot_grad, phi_param)


def solution(mesh):
    return jax.shard_map(
        functools.partial(per_device, mesh.shape["seq"], mesh.shape["batch"]),
        mesh=mesh,
        in_specs=(
            P("batch", "seq", None),
            P("batch", "seq", None),
            P("batch", "seq", None),
            P("seq", None),
        ),
        out_specs=(P("batch", "seq", None), P("seq", None)),
        check_vma=False,
    )
```

profile of v0, /device:TPU:0, one launch (start us, length us, event | category | flops | bytes accessed | tf_op | source)
XLA Modules:
  0.0 37.4 jit_solution(14594746357890213466)
XLA Ops:
  0.6 34.8 %shard_map.59 = (bf16[1024,1024]{1,0:T(8,128)(2,1)S(1)}, f32[128,256]{1,0:T(8,128)S(1)}) custom-call(bf16[1024,1024]{1,0:T(8,128)(2,1)} %bitcast.6, bf16[1024,256]{1,0:T(8,128)(2,1)} %bitcast.7, bf16[32,1024]{1,0:T(8,128)(2,1)} %bitcast.8, bf16[4,32,256]{2,1,0:T(8,128)(2,1)} %bitcast.9), custom_call_target="tpu_custom_call" | custom-call | tf_op jit(solution)/shard_map/pallas_call | solution.py:271
  35.4 1.3 %copy.8 = bf16[1,1024,1024]{2,1,0:T(8,128)(2,1)} copy(bf16[1,1024,1024]{2,1,0:T(8,128)(2,1)S(1)} %bitcast.5) | data formatting | bytes 4194304
  36.8 0.7 %copy.9 = f32[128,256]{1,0:T(8,128)} copy(f32[128,256]{1,0:T(8,128)S(1)} %get-tuple-element.9) | data formatting | bytes 262144
where the time goes:
time: 37.6 us; the launch traced here: 37.4 us
  Pallas kernels  34.8 us (93%)
  local copies, waits for them, and re-layouts  1.98 us (5%)
  between operations  0.64 us (2%)
    pallas_call x1, Pallas kernels, fused(): pl.pallas_call(functools.partial(fused_kernel, n, scale), out_shape=(jax....  34.8 us
    unnamed x2, local copies, waits for them, and re-layouts  1.98 us

commit v1 on v0

v1 whole, which is shorter than its diff:
```python
import functools

import jax
import jax.numpy as jnp
from jax import lax
from jax.experimental import pallas as pl
from jax.experimental.pallas import tpu as pltpu
from jax.sharding import PartitionSpec as P

MESH = pl.DeviceIdType.MESH
F32 = jnp.float32
BF16 = jnp.bfloat16
PIECES = 2
LAG = 0.5


def fused_kernel(
    n, scale, tok_hbm, log_hbm, slot_hbm, phi_hbm, tok_out, phi_out,
    tok, log, raw, raw_low, wg, gath, phig, ends, dots, gam, disp, lg, tokt,
    mass, mass_in, part, part_low, recv_a, sum_a, low_a, recv_b, sum_b, low_b, recv_c, fin,
    load_sem, ag_send, ag_recv, fw_send, fw_recv, en_send, en_recv, do_send, do_recv, ga_send, ga_recv,
    ph_send, ph_recv, pa_send, pa_recv, m_send, m_recv,
    a_send, a_recv, b_send, b_recv, c_send, c_recv, d_send, d_recv,
):
    me = lax.axis_index("seq")
    bat = lax.axis_index("batch")
    half = n // 2
    place = me // 2
    col = me % 2
    twin = me + 1 - 2 * col
    bat_a = bat + 1 - 2 * (bat % 2)
    bat_b = (bat + 2) % 4
    bat_c = (bat_a + 2) % 4
    keep_a = bat % 2
    keep_b = bat // 2
    mates = ((bat_a, 1 - keep_a, keep_b), (bat_b, keep_a, 1 - keep_b), (bat_c, 1 - keep_a, 1 - keep_b))
    rows = tok.shape[0]
    slots = log.shape[1]
    step = min(256, rows)
    steps = rows // step
    large = 2 * step if rows % (2 * step) == 0 else step
    pieces, span = gath.shape[0], gath.shape[3]
    own = tok.shape[1] // n
    quarter = own // 4
    group = n // 2
    owners = [[j for j in range(n) if (n // 4 <= j < n - n // 4) == bool(g)] for g in range(2)]

    def remote(src, dst, send, recv, seq_at, bat_at):
        return pltpu.make_async_remote_copy(
            src_ref=src, dst_ref=dst, send_sem=send, recv_sem=recv,
            device_id=(seq_at, bat_at), device_id_type=MESH,
        )

    def chunk(i):
        return pl.ds(pl.multiple_of(i * step, step), step)

    def wide(i):
        return pl.ds(pl.multiple_of(i * large, large), large)

    load_slot = [
        pltpu.make_async_copy(slot_hbm.at[:, q * span : (q + 1) * span], gath.at[q, me], load_sem.at[3 + q])
        for q in range(pieces)
    ]
    load_log = pltpu.make_async_copy(log_hbm, log, load_sem.at[0])
    load_phi = pltpu.make_async_copy(phi_hbm.at[keep_a], phig.at[me, keep_a], load_sem.at[1])
    load_tok = pltpu.make_async_copy(tok_hbm, tok, load_sem.at[2])
    for load in load_slot:
        load.start()
    load_log.start()
    load_tok.start()
    load_phi.start()

    barrier = pltpu.get_barrier_semaphore()
    for k in range(1, n):
        pl.semaphore_signal(barrier, inc=1, device_id=((me + k) % n, bat), device_id_type=MESH)
    for other in (bat_a, bat_b, bat_c):
        pl.semaphore_signal(barrier, inc=1, device_id=(me, other), device_id_type=MESH)
    pl.semaphore_wait(barrier, n - 1 + 3)

    def inside(p):
        return (p >= 0) & (p < half)

    def to_twin(p, q):
        shard = gath.at[q, 2 * p + col]
        return remote(shard, shard, fw_send, fw_recv.at[q], twin, bat)

    def along(p, target, q):
        shard = gath.at[q, 2 * p + col]
        return remote(shard, shard, ag_send, ag_recv.at[p, q], 2 * target + col, bat)

    def send_own():
        for q in range(pieces):
            load_slot[q].wait()
            to_twin(place, q).start()
            for dist in range(1, half):
                for sign in (1, -1):
                    @pl.when(inside(place + sign * dist))
                    def _(dist=dist, sign=sign, q=q):
                        along(place, place + sign * dist, q).start()

    def arrive(dist, sign, q):
        p = place + sign * dist

        @pl.when(inside(p))
        def _():
            along(p, p, q).wait_recv()
            to_twin(p, q).start()

    def whole(ref, sem):
        return remote(ref, ref, sem, sem, me, bat_a)

    @pl.when(keep_a == 0)
    def _():
        send_own()

    load_log.wait()

    def peak_step(i, top):
        return jnp.maximum(top, jnp.max(log[chunk(i), :].astype(F32), axis=0, keepdims=True))

    peak = lax.fori_loop(0, steps, peak_step, jnp.full((1, slots), -jnp.inf, F32))

    def exp_step(i, acc):
        values = jnp.exp(log[chunk(i), :].astype(F32) - peak)
        raw[chunk(i), :] = values
        raw_low[chunk(i), :] = values.astype(BF16)
        return acc + jnp.sum(values, axis=0, keepdims=True)

    total = lax.fori_loop(0, steps, exp_step, jnp.zeros((1, slots), F32))
    ends[me, 0:1, :] = peak
    ends[me, 1:2, :] = total
    for k in range(1, n):
        remote(ends.at[me], ends.at[me], en_send, en_recv, (me + k) % n, bat).start()

    @pl.when(keep_a == 1)
    def _():
        send_own()

    load_tok.wait()

    def turn_step(i, carry):
        tokt[:, chunk(i)] = tok[chunk(i), :].T
        return carry

    lax.fori_loop(0, steps, turn_step, 0)

    def terms_of(weights, g, at, put):
        j = owners[g][at]
        terms = jnp.dot(tokt[own * j : own * (j + 2), :], weights[...], preferred_element_type=F32)
        for side in range(2):
            for qa in range(2):
                for qb in range(2):
                    first = own * side + (2 * qa + qb) * quarter
                    put(g, qa, qb, at + side, terms[first : first + quarter, :])

    def put_mass(g, qa, qb, at, block):
        mass[g, qa, qb, at] = block.astype(BF16)


    def mass_task(g, at):
        terms_of(raw_low, g, at, put_mass)
        if at + 2 == group:
            for k, (mate, qa, qb) in enumerate(mates):
                remote(mass.at[g, qa, qb], mass_in.at[k, g], m_send, m_recv, me, mate).start()

    tasks = [(g, at) for g in range(2) for at in range(0, group, 2)]
    coming = sorted((q + LAG * (dist - 1), dist, q) for q in range(pieces) for dist in range(1, half))
    for _, dist, q in coming:
        if tasks:
            mass_task(*tasks.pop(0))
        for sign in (1, -1):
            arrive(dist, sign, q)
    for task in tasks:
        mass_task(*task)

    whole(ends.at[: n - 1], en_recv).wait_recv()
    peaks = ends[:, 0:1, :]
    col_peak = jnp.max(peaks, axis=0)
    col_total = jnp.sum(ends[:, 1:2, :] * jnp.exp(peaks - col_peak), axis=0)
    factor = jnp.exp(peak - col_peak) / col_total

    dot = jnp.zeros((1, slots), F32)
    for q in range(pieces):
        whole(gath.at[q, :half], fw_recv.at[q]).wait_recv()

        def wg_step(i, acc, q=q):
            values = lax.dot_general(
                tok[wide(i), q * span : (q + 1) * span], gath[q].reshape(slots, span),
                (((1,), (1,)), ((), ())), preferred_element_type=F32,
            )
            if q:
                values = values + wg[wide(i), :]
            wg[wide(i), :] = values
            if q == pieces - 1:
                acc = acc + jnp.sum(values * raw[wide(i), :], axis=0, keepdims=True)
            return acc

        dot = lax.fori_loop(0, rows // large, wg_step, dot)

    dots[me] = factor * dot
    for k in range(1, n):
        remote(dots.at[me], dots.at[me], do_send, do_recv, (me + k) % n, bat).start()
    load_phi.wait()
    for k in range(1, n):
        remote(phig.at[me, keep_a], phig.at[me, keep_a], ph_send, ph_recv, (me + k) % n, bat).start()

    center = dot / total

    def center_step(i, carry):
        lg[chunk(i), :] = (raw[chunk(i), :] * factor * (wg[chunk(i), :] - center)).astype(BF16)
        return carry

    lax.fori_loop(0, steps, center_step, 0)

    def put_part(g, qa, qb, at, block):
        part[g, qa, qb, at] = block
        part_low[g, qa, qb, at] = block.astype(BF16)

    moves_a = []
    for g in range(2):
        for at in range(0, group, 2):
            terms_of(lg, g, at, put_part)
        moves_a.append(remote(part_low.at[g, 1 - keep_a], recv_a.at[g], a_send, a_recv.at[g], me, bat_a))
        moves_a[-1].start()
    moves_b = []
    for g in range(2):
        moves_a[g].wait_recv()
        for qb in range(2):
            for at in range(group):
                block = part[g, keep_a, qb, at] + recv_a[g, qb, at].astype(F32)
                sum_a[g, qb, at] = block
                low_a[g, qb, at] = block.astype(BF16)
        moves_b.append(remote(low_a.at[g, 1 - keep_b], recv_b.at[g], b_send, b_recv.at[g], me, bat_b))
        moves_b[-1].start()

    whole(dots.at[: n - 1], do_recv).wait_recv()
    col_dot = jnp.sum(dots[...], axis=0)
    gam[0] = factor * (center - col_dot)
    for k, (mate, _, _) in enumerate(mates):
        remote(gam.at[0], gam.at[1 + k], ga_send, ga_recv, me, mate).start()

    def grad_step(i, carry):
        weights = raw[chunk(i), :] * factor
        grads = weights * (wg[chunk(i), :] - col_dot)
        disp[chunk(i), :] = weights.astype(BF16)
        lg[chunk(i), :] = grads.astype(BF16)
        return carry

    lax.fori_loop(0, steps, grad_step, 0)

    whole(mass_in, m_recv).wait_recv()
    whole(gam.at[1:], ga_recv).wait_recv()

    def share_move(g, at):
        j = owners[g][at]
        return remote(low_b.at[g, at], recv_c.at[me], c_send, c_recv, j, bat)

    for g in range(2):
        moves_b[g].wait_recv()
        for at in range(group):
            block = sum_a[g, keep_b, at] + recv_b[g, at].astype(F32)
            block = block + mass[g, keep_a, keep_b, at].astype(F32) * gam[0]
            for k in range(3):
                block = block + mass_in[k, g, at].astype(F32) * gam[1 + k]
            sum_b[owners[g][at]] = block
            low_b[g, at] = block.astype(BF16)
        for at in range(group):
            @pl.when(me != owners[g][at])
            def _(g=g, at=at):
                share_move(g, at).start()

    whole(phig.at[: n - 1, 0], ph_recv).wait_recv()
    phi_a = remote(phig.at[:, keep_a], phig.at[:, keep_a], pa_send, pa_recv, me, bat_a)
    phi_a.start()
    phi_a.wait_recv()
    phi_full = phig.reshape(n * own, slots)

    def out_step(i, carry):
        for q in range(pieces):
            values = jnp.dot(disp[wide(i), :], gath[q].reshape(slots, span), preferred_element_type=F32)
            values = values + lax.dot_general(
                lg[wide(i), :], phi_full[q * span : (q + 1) * span, :],
                (((1,), (1,)), ((), ())), preferred_element_type=F32,
            )
            tok_out[wide(i), q * span : (q + 1) * span] = (scale * values).astype(BF16)
        return carry

    lax.fori_loop(0, rows // large, out_step, 0)

    share = sum_b[me]
    whole(recv_c.at[: n - 1], c_recv).wait_recv()
    for k in range(1, n):
        share = share + recv_c[(me - k + n) % n].astype(F32)
    mine = 2 * keep_a + keep_b
    fin[mine] = share
    for k, other in enumerate((bat_c, bat_b, bat_a)):
        remote(fin.at[mine], fin.at[mine], d_send, d_recv, me, other).start()
    whole(fin.at[:3], d_recv).wait_recv()
    phi_out[...] = fin[...].reshape(own, slots)

    for ref, sem in (
        (gath.at[:, : half - 1], ag_send), (gath.at[:, :half], fw_send), (ends.at[: n - 1], en_send), (dots.at[: n - 1], do_send),
        (gam.at[1:], ga_send), (phig.at[: n - 1, 0], ph_send), (phig.at[:, 0], pa_send), (mass_in, m_send),
        (recv_a, a_send), (recv_b, b_send), (recv_c.at[: n - 1], c_send), (fin.at[:3], d_send),
    ):
        whole(ref, sem).wait_send()


def fused(n, tokens, logits, slot_grad, phi_param):
    rows, width = tokens.shape
    slots = logits.shape[1]
    own = width // n
    quarter = own // 4
    half = n // 2
    scale = float(n * rows // 16)
    dma = pltpu.SemaphoreType.DMA
    hbm = pl.BlockSpec(memory_space=pltpu.HBM)
    return pl.pallas_call(
        functools.partial(fused_kernel, n, scale),
        out_shape=(
            jax.ShapeDtypeStruct((rows, width), BF16),
            jax.ShapeDtypeStruct((own, slots), F32),
        ),
        in_specs=[hbm] * 4,
        out_specs=(pl.BlockSpec(memory_space=pltpu.VMEM), pl.BlockSpec(memory_space=pltpu.VMEM)),
        scratch_shapes=[
            pltpu.VMEM((rows, width), BF16),
            pltpu.VMEM((rows, slots), BF16),
            pltpu.VMEM((rows, slots), F32),
            pltpu.VMEM((rows, slots), BF16),
            pltpu.VMEM((rows, slots), F32),
            pltpu.VMEM((PIECES, n, slots // n, width // PIECES), BF16),
            pltpu.VMEM((n, 2, own // 2, slots), BF16),
            pltpu.VMEM((n, 2, slots), F32),
            pltpu.VMEM((n, 1, slots), F32),
            pltpu.VMEM((4, 1, slots), F32),
            pltpu.VMEM((rows, slots), BF16),
            pltpu.VMEM((rows, slots), BF16),
            pltpu.VMEM((width, rows), BF16),
            pltpu.VMEM((2, 2, 2, half, quarter, slots), BF16),
            pltpu.VMEM((3, 2, half, quarter, slots), BF16),
            pltpu.VMEM((2, 2, 2, half, quarter, slots), F32),
            pltpu.VMEM((2, 2, 2, half, quarter, slots), BF16),
            pltpu.VMEM((2, 2, half, quarter, slots), BF16),
            pltpu.VMEM((2, 2, half, quarter, slots), F32),
            pltpu.VMEM((2, 2, half, quarter, slots), BF16),
            pltpu.VMEM((2, half, quarter, slots), BF16),
            pltpu.VMEM((n, quarter, slots), F32),
            pltpu.VMEM((2, half, quarter, slots), BF16),
            pltpu.VMEM((n, quarter, slots), BF16),
            pltpu.VMEM((4, quarter, slots), F32),
            dma((3 + PIECES,)),
            dma, dma((half, PIECES)), dma, dma((PIECES,)),
            dma, dma, dma, dma, dma, dma,
            dma, dma, dma, dma, dma, dma,
            dma, dma((2,)), dma, dma((2,)),
            dma, dma, dma, dma,
        ],
        compiler_params=pltpu.CompilerParams(
            collective_id=0, has_side_effects=True, vmem_limit_bytes=52_000_000
        ),
    )(*[
        pltpu.with_memory_space_constraint(x, pltpu.HBM)
        for x in (tokens, logits, slot_grad, phi_param.reshape(2, own // 2, slots))
    ])


def plain(tokens, logits, slot_grad, phi_param):
    inputs = tokens[0]
    scores = logits[0].astype(jnp.float32)
    upstream, phi_full = (
        lax.all_gather(slot_grad[0], "seq", axis=0, tiled=True),
        lax.all_gather(phi_param, "seq", axis=0, tiled=True),
    )
    weight_grad = lax.dot_general(
        inputs, upstream, (((1,), (1,)), ((), ())), preferred_element_type=jnp.float32
    )
    col_peak = lax.pmax(jnp.max(scores, axis=0, keepdims=True), "seq")
    raw_weights = jnp.exp(scores - col_peak)
    col_total = lax.psum(jnp.sum(raw_weights, axis=0, keepdims=True), "seq")
    dispatch = raw_weights / col_total
    col_dot = lax.psum(jnp.sum(dispatch * weight_grad, axis=0, keepdims=True), "seq")
    logit_grad = (dispatch * (weight_grad - col_dot)).astype(jnp.bfloat16)
    dispatch_low = dispatch.astype(jnp.bfloat16)
    grad_scale = float(lax.axis_size("seq") * inputs.shape[0] // 16)
    token_sum = jnp.dot(dispatch_low, upstream, preferred_element_type=jnp.float32)
    token_sum = token_sum + lax.dot_general(
        logit_grad, phi_full, (((1,), (1,)), ((), ())), preferred_element_type=jnp.float32
    )
    token_grad = (grad_scale * token_sum).astype(jnp.bfloat16)[None]
    phi_terms = lax.dot_general(
        inputs, logit_grad, (((0,), (0,)), ((), ())), preferred_element_type=jnp.float32
    )
    phi_share = lax.psum_scatter(phi_terms, "seq", scatter_dimension=0, tiled=True)
    phi_grad = lax.psum(phi_share, "batch")
    return (token_grad, phi_grad)


def per_device(n, batches, tokens, logits, slot_grad, phi_param):
    own, slots = phi_param.shape
    if batches == 4 and n % 8 == 0 and slot_grad.shape[1] % 16 == 0 and own % 128 == 0 and slots % 128 == 0 and tokens.shape[1] % 256 == 0:
        token_grad, phi_grad = fused(n, tokens[0], logits[0], slot_grad[0], phi_param)
        return token_grad[None], phi_grad
    return plain(tokens, logits, slot_grad, phi_param)


def solution(mesh):
    return jax.shard_map(
        functools.partial(per_device, mesh.shape["seq"], mesh.shape["batch"]),
        mesh=mesh,
        in_specs=(
            P("batch", "seq", None),
            P("batch", "seq", None),
            P("batch", "seq", None),
            P("seq", None),
        ),
        out_specs=(P("batch", "seq", None), P("seq", None)),
        check_vma=False,
    )
```

time: 37.6 us -> 35 us (0.931)
  Pallas kernels: 34.8 us -> 32.2 us
    pallas_call x1, Pallas kernels: 34.8 us -> 32.2 us  [fused(): pl.pallas_call(functools.partial(fused_kernel, n, scale), out_shape=(jax....]
where the time goes in v1:
time: 35 us; the launch traced here: 34.8 us
  Pallas kernels  32.2 us (92%)
  local copies, waits for them, and re-layouts  1.98 us (6%)
  between operations  0.64 us (2%)
    pallas_call x1, Pallas kernels, fused(): pl.pallas_call(functools.partial(fused_kernel, n, scale), out_shape=(jax....  32.2 us
    unnamed x2, local copies, waits for them, and re-layouts  1.98 us

profile of v1, /device:TPU:0, one launch (start us, length us, event | category | flops | bytes accessed | tf_op | source)
XLA Modules:
  0.0 34.8 jit_solution(11041507085416990599)
XLA Ops:
  0.6 32.2 %shard_map.59 = (bf16[1024,1024]{1,0:T(8,128)(2,1)S(1)}, f32[128,256]{1,0:T(8,128)S(1)}) custom-call(bf16[1024,1024]{1,0:T(8,128)(2,1)} %bitcast.6, bf16[1024,256]{1,0:T(8,128)(2,1)} %bitcast.7, bf16[32,1024]{1,0:T(8,128)(2,1)} %bitcast.8, bf16[2,64,256]{2,1,0:T(8,128)(2,1)} %bitcast.9), custom_call_target="tpu_custom_call" | custom-call | tf_op jit(solution)/shard_map/pallas_call | solution.py:318
  32.8 1.3 %copy.8 = bf16[1,1024,1024]{2,1,0:T(8,128)(2,1)} copy(bf16[1,1024,1024]{2,1,0:T(8,128)(2,1)S(1)} %bitcast.5) | data formatting | bytes 4194304
  34.2 0.7 %copy.9 = f32[128,256]{1,0:T(8,128)} copy(f32[128,256]{1,0:T(8,128)S(1)} %get-tuple-element.9) | data formatting | bytes 262144

commit v2 on v1

--- a/solution.py
+++ b/solution.py
@@ -12,6 +12,10 @@
 BF16 = jnp.bfloat16
 PIECES = 2
 LAG = 0.5
+WGROWS = 512
+CUTS = 4
+LIMIT = 6_000_000
+OUTROWS = 512
 
 
 def fused_kernel(
@@ -38,7 +42,8 @@
     slots = log.shape[1]
     step = min(256, rows)
     steps = rows // step
-    large = 2 * step if rows % (2 * step) == 0 else step
+    large = min(WGROWS, rows)
+    tall = min(OUTROWS, rows)
     pieces, span = gath.shape[0], gath.shape[3]
     own = tok.shape[1] // n
     quarter = own // 4
@@ -56,6 +61,9 @@
 
     def wide(i):
         return pl.ds(pl.multiple_of(i * large, large), large)
+
+    def band(i):
+        return pl.ds(pl.multiple_of(i * tall, tall), tall)
 
     load_slot = [
         pltpu.make_async_copy(slot_hbm.at[:, q * span : (q + 1) * span], gath.at[q, me], load_sem.at[3 + q])
@@ -197,14 +205,19 @@
 
         dot = lax.fori_loop(0, rows // large, wg_step, dot)
 
+    center = dot / total
     dots[me] = factor * dot
+    gam[0, 0:1, :] = factor
+    gam[0, 1:2, :] = center
     for k in range(1, n):
         remote(dots.at[me], dots.at[me], do_send, do_recv, (me + k) % n, bat).start()
+    for k, (mate, _, _) in enumerate(mates):
+        for other in range(n):
+            remote(dots.at[me], dots.at[(1 + k) * n + me], do_send, do_recv, (me + other) % n, mate).start()
+        remote(gam.at[0], gam.at[1 + k], ga_send, ga_recv, me, mate).start()
     load_phi.wait()
     for k in range(1, n):
         remote(phig.at[me, keep_a], phig.at[me, keep_a], ph_send, ph_recv, (me + k) % n, bat).start()
-
-    center = dot / total
 
     def center_step(i, carry):
         lg[chunk(i), :] = (raw[chunk(i), :] * factor * (wg[chunk(i), :] - center)).astype(BF16)
@@ -233,23 +246,11 @@
         moves_b.append(remote(low_a.at[g, 1 - keep_b], recv_b.at[g], b_send, b_recv.at[g], me, bat_b))
         moves_b[-1].start()
 
-    whole(dots.at[: n - 1], do_recv).wait_recv()
-    col_dot = jnp.sum(dots[...], axis=0)
-    gam[0] = factor * (center - col_dot)
-    for k, (mate, _, _) in enumerate(mates):
-        remote(gam.at[0], gam.at[1 + k], ga_send, ga_recv, me, mate).start()
-
-    def grad_step(i, carry):
-        weights = raw[chunk(i), :] * factor
-        grads = weights * (wg[chunk(i), :] - col_dot)
-        disp[chunk(i), :] = weights.astype(BF16)
-        lg[chunk(i), :] = grads.astype(BF16)
-        return carry
-
-    lax.fori_loop(0, steps, grad_step, 0)
-
+    whole(dots.at[: 4 * n - 1], do_recv).wait_recv()
+    whole(gam.at[1:], ga_recv).wait_recv()
+    col_dot = [jnp.sum(dots[k * n : (k + 1) * n], axis=0) for k in range(4)]
+    shift = [gam[k, 0:1, :] * (gam[k, 1:2, :] - col_dot[k]) for k in range(4)]
     whole(mass_in, m_recv).wait_recv()
-    whole(gam.at[1:], ga_recv).wait_recv()
 
     def share_move(g, at):
         j = owners[g][at]
@@ -259,9 +260,9 @@
         moves_b[g].wait_recv()
         for at in range(group):
             block = sum_a[g, keep_b, at] + recv_b[g, at].astype(F32)
-            block = block + mass[g, keep_a, keep_b, at].astype(F32) * gam[0]
+            block = block + mass[g, keep_a, keep_b, at].astype(F32) * shift[0]
             for k in range(3):
-                block = block + mass_in[k, g, at].astype(F32) * gam[1 + k]
+                block = block + mass_in[k, g, at].astype(F32) * shift[1 + k]
             sum_b[owners[g][at]] = block
             low_b[g, at] = block.astype(BF16)
         for at in range(group):
@@ -272,38 +273,59 @@
     whole(phig.at[: n - 1, 0], ph_recv).wait_recv()
     phi_a = remote(phig.at[:, keep_a], phig.at[:, keep_a], pa_send, pa_recv, me, bat_a)
     phi_a.start()
+
+    def grad_step(i, carry):
+        weights = raw[chunk(i), :] * factor
+        grads = weights * (wg[chunk(i), :] - col_dot[0])
+        disp[chunk(i), :] = weights.astype(BF16)
+        lg[chunk(i), :] = grads.astype(BF16)
+        return carry
+
+    lax.fori_loop(0, steps, grad_step, 0)
     phi_a.wait_recv()
     phi_full = phig.reshape(n * own, slots)
 
     def out_step(i, carry):
         for q in range(pieces):
-            values = jnp.dot(disp[wide(i), :], gath[q].reshape(slots, span), preferred_element_type=F32)
+            values = jnp.dot(disp[band(i), :], gath[q].reshape(slots, span), preferred_element_type=F32)
             values = values + lax.dot_general(
-                lg[wide(i), :], phi_full[q * span : (q + 1) * span, :],
+                lg[band(i), :], phi_full[q * span : (q + 1) * span, :],
                 (((1,), (1,)), ((), ())), preferred_element_type=F32,
             )
-            tok_out[wide(i), q * span : (q + 1) * span] = (scale * values).astype(BF16)
+            tok_out[band(i), q * span : (q + 1) * span] = (scale * values).astype(BF16)
         return carry
 
-    lax.fori_loop(0, rows // large, out_step, 0)
+    lax.fori_loop(0, rows // tall, out_step, 0)
 
     share = sum_b[me]
     whole(recv_c.at[: n - 1], c_recv).wait_recv()
     for k in range(1, n):
         share = share + recv_c[(me - k + n) % n].astype(F32)
     mine = 2 * keep_a + keep_b
-    fin[mine] = share
+    fin[mine] = share.astype(BF16)
     for k, other in enumerate((bat_c, bat_b, bat_a)):
         remote(fin.at[mine], fin.at[mine], d_send, d_recv, me, other).start()
     whole(fin.at[:3], d_recv).wait_recv()
-    phi_out[...] = fin[...].reshape(own, slots)
+    phi_out[...] = fin[...].astype(F32).reshape(own, slots)
 
     for ref, sem in (
-        (gath.at[:, : half - 1], ag_send), (gath.at[:, :half], fw_send), (ends.at[: n - 1], en_send), (dots.at[: n - 1], do_send),
+        (gath.at[:, : half - 1], ag_send), (gath.at[:, :half], fw_send), (ends.at[: n - 1], en_send), (dots.at[: 4 * n - 1], do_send),
         (gam.at[1:], ga_send), (phig.at[: n - 1, 0], ph_send), (phig.at[:, 0], pa_send), (mass_in, m_send),
         (recv_a, a_send), (recv_b, b_send), (recv_c.at[: n - 1], c_send), (fin.at[:3], d_send),
     ):
         whole(ref, sem).wait_send()
+
+
+def place_kernel(tok_in, phi_in, tok_hbm, phi_hbm, sem):
+    block = tok_in.shape[0] // CUTS
+    moves = [pltpu.make_async_copy(phi_in, phi_hbm, sem.at[CUTS])]
+    for k in range(CUTS):
+        part = pl.ds(k * block, block)
+        moves.append(pltpu.make_async_copy(tok_in.at[part], tok_hbm.at[part], sem.at[k]))
+    for move in moves:
+        move.start()
+    for move in moves:
+        move.wait()
 
 
 def fused(n, tokens, logits, slot_grad, phi_param):
@@ -315,7 +337,7 @@
     scale = float(n * rows // 16)
     dma = pltpu.SemaphoreType.DMA
     hbm = pl.BlockSpec(memory_space=pltpu.HBM)
-    return pl.pallas_call(
+    grads = pl.pallas_call(
         functools.partial(fused_kernel, n, scale),
         out_shape=(
             jax.ShapeDtypeStruct((rows, width), BF16),
@@ -332,8 +354,8 @@
             pltpu.VMEM((PIECES, n, slots // n, width // PIECES), BF16),
             pltpu.VMEM((n, 2, own // 2, slots), BF16),
             pltpu.VMEM((n, 2, slots), F32),
-            pltpu.VMEM((n, 1, slots), F32),
-            pltpu.VMEM((4, 1, slots), F32),
+            pltpu.VMEM((4 * n, 1, slots), F32),
+            pltpu.VMEM((4, 2, slots), F32),
             pltpu.VMEM((rows, slots), BF16),
             pltpu.VMEM((rows, slots), BF16),
             pltpu.VMEM((width, rows), BF16),
@@ -348,7 +370,7 @@
             pltpu.VMEM((n, quarter, slots), F32),
             pltpu.VMEM((2, half, quarter, slots), BF16),
             pltpu.VMEM((n, quarter, slots), BF16),
-            pltpu.VMEM((4, quarter, slots), F32),
+            pltpu.VMEM((4, quarter, slots), BF16),
             dma((3 + PIECES,)),
             dma, dma((half, PIECES)), dma, dma((PIECES,)),
             dma, dma, dma, dma, dma, dma,
@@ -363,6 +385,17 @@
         pltpu.with_memory_space_constraint(x, pltpu.HBM)
         for x in (tokens, logits, slot_grad, phi_param.reshape(2, own // 2, slots))
     ])
+    return pl.pallas_call(
+        place_kernel,
+        out_shape=(
+            jax.ShapeDtypeStruct((rows, width), BF16),
+            jax.ShapeDtypeStruct((own, slots), F32),
+        ),
+        in_specs=[pl.BlockSpec(memory_space=pltpu.VMEM)] * 2,
+        out_specs=(hbm, hbm),
+        scratch_shapes=[dma((CUTS + 1,))],
+        compiler_params=pltpu.CompilerParams(vmem_limit_bytes=LIMIT),
+    )(*grads)
 
 
 def plain(tokens, logits, slot_grad, phi_param):

time: 35 us -> 32.6 us (0.931)
  local copies, waits for them, and re-layouts: 1.98 us -> 0 us
  Pallas kernels: 32.2 us -> 31.8 us
    unnamed x2 -> x0, local copies, waits for them, and re-layouts: 1.98 us -> none
    pallas_call x1, Pallas kernels: 32.2 us -> 30.4 us  [fused(): pl.pallas_call(functools.partial(fused_kernel, n, scale), out_shape=(jax....]
    pallas_call x0 -> x1, Pallas kernels: none -> 1.4 us  [fused(): pl.pallas_call(place_kernel, out_shape=(jax.ShapeDtypeStruct((rows, width...]
where the time goes in v2:
time: 32.6 us; the launch traced here: 32.4 us
  Pallas kernels  31.8 us (98%)
  between operations  0.64 us (2%)
    pallas_call x1, Pallas kernels, fused(): pl.pallas_call(functools.partial(fused_kernel, n, scale), out_shape=(jax....  30.4 us
    pallas_call x1, Pallas kernels, fused(): pl.pallas_call(place_kernel, out_shape=(jax.ShapeDtypeStruct((rows, width...  1.4 us

profile of v2, /device:TPU:0, one launch (start us, length us, event | category | flops | bytes accessed | tf_op | source)
XLA Modules:
  0.0 32.4 jit_solution(398370227674369106)
XLA Ops:
  0.6 30.4 %shard_map.59 = (bf16[1024,1024]{1,0:T(8,128)(2,1)S(1)}, f32[128,256]{1,0:T(8,128)S(1)}) custom-call(bf16[1024,1024]{1,0:T(8,128)(2,1)} %bitcast.5, bf16[1024,256]{1,0:T(8,128)(2,1)} %bitcast.6, bf16[32,1024]{1,0:T(8,128)(2,1)} %bitcast.7, bf16[2,64,256]{2,1,0:T(8,128)(2,1)} %bitcast.8), custom_call_target="tpu_custom_call" | custom-call | tf_op jit(solution)/shard_map/pallas_call | solution.py:340
  31.0 1.4 %shard_map.60 = (bf16[1024,1024]{1,0:T(8,128)(2,1)}, f32[128,256]{1,0:T(8,128)}) custom-call(bf16[1024,1024]{1,0:T(8,128)(2,1)S(1)} %get-tuple-element.6.tok_in, f32[128,256]{1,0:T(8,128)S(1)} %get-tuple-element.7.phi_in), custom_call_target="tpu_custom_call" | custom-call | tf_op jit(solution)/shard_map/pallas_call | solution.py:388
